TPU v7x, 32 devices: a whole 2x2x4 slice. The times are simulated.
32 devices in a mesh: blk: 8 (over z, y), pix: 4 (over x, core).
Axes of the slice: x: 2, y: 2, z: 4, core: 2. Of those that a mesh axis runs over, the one named last changes fastest.
Arguments:
- pixels: bfloat16 [32768, 224], P(('blk', 'pix')), may hold values from -6 to 6
- bundles: bfloat16 [16, 224, 64], P('blk'), may hold values from -0.375 to 0.375
- assign: int32 [32768, 1], P(('blk', 'pix')), may hold values from 0 to 15; in each aligned block of 1024 rows (0 to 1023, 1024 to 2047, ...) at most 128 rows name the same one
Outputs:
- abundances: float32 [32768, 64], P(('blk', 'pix'))
- residual_energy: float32 [8, 16], P('blk')
Inputs may be any that keep to these rules, and one draw needn't show every extreme that they name: `assign`: among the 1024 rows of one device no bundle is named more than 128 times; in every draw some device names some bundle exactly 128 times; every bundle is named somewhere.
All inputs are finite; a program needn't handle non-finite values. Where the computation divides by a largest or mean magnitude, that divisor is 1e-20 or more.
Results may differ from a plain program's by a relative error of at most 0.0003.
Values may be sent and summed in bfloat16 or wider, within the bound.
A program may use at most 64 MiB of HBM per device.

v0:
```python
import jax
import jax.numpy as jnp
from jax import lax
from jax.sharding import PartitionSpec as P

ITERS = 8


sum_weight = 0.015625


def make_slots(assign, count, cap):
    labels = assign[:, 0]
    onehot = (labels[:, None] == jnp.arange(count, dtype=jnp.int32)[None, :]).astype(jnp.int32)
    ranked = jnp.sum(jnp.cumsum(onehot, axis=0) * onehot, axis=1) - 1
    return labels * cap + ranked


def gram_of(spectra):
    gram = (
        jnp.einsum("nbm,nbk->nmk", spectra, spectra, preferred_element_type=jnp.float32)
        + sum_weight
    )
    step = 1.0 / jnp.max(jnp.sum(jnp.abs(gram), axis=2), axis=1)
    return (gram, step)


def solve(blocks, spectra, gram, step):
    target = (
        jnp.einsum("nsb,nbm->nsm", blocks, spectra, preferred_element_type=jnp.float32) + sum_weight
    )

    def sweep(index, state):
        grad = jnp.einsum("nsm,nmk->nsk", state, gram, precision=lax.Precision.HIGHEST)
        return jnp.maximum(state - step[:, None, None] * (grad - target), 0.0)

    state = lax.fori_loop(0, ITERS, sweep, jnp.zeros_like(target))
    fitted = jnp.einsum(
        "nsm,nbm->nsb", state, spectra.astype(jnp.float32), precision=lax.Precision.HIGHEST
    )
    misfit = blocks.astype(jnp.float32) - fitted
    return (state, jnp.sum(misfit * misfit, axis=-1))


def per_device(pixels, bundles, assign):
    rows, bands = pixels.shape
    width = bundles.shape[2]
    owned = bundles.shape[0]
    count = lax.axis_size("blk") * owned
    cap = 2 * rows // count
    slots = make_slots(assign, count, cap)
    flat = jnp.zeros((count * cap, bands), jnp.bfloat16).at[slots].set(pixels)
    buckets = flat.reshape(count, cap, bands)
    valid = jnp.zeros((count * cap,), jnp.float32).at[slots].set(1.0).reshape(count, cap)
    piece = lax.all_gather(bundles, "blk", axis=0, tiled=True)
    grams, steps = gram_of(piece)
    state, misfit = solve(buckets, piece, grams, steps)
    chosen = state.reshape(count * cap, width)[slots]
    scale = bands * rows * lax.axis_size("pix") / count
    energy = jnp.sum(misfit * valid / scale, axis=1)
    total = lax.psum(energy, "pix")
    return (chosen, total[None, :])


def solution(mesh):
    placed = (P(("blk", "pix"), None), P("blk", None, None), P(("blk", "pix"), None))
    return jax.shard_map(
        per_device,
        mesh=mesh,
        in_specs=placed,
        out_specs=(P(("blk", "pix"), None), P("blk", None)),
        check_vma=False,
    )
```

profile of v0, /device:TPU:0, one launch (start us, length us, event | category | flops | bytes accessed | tf_op | source)
XLA Modules:
  0.0 69.8 jit_solution(9833450703897635159)
XLA Ops:
  0.6 0.7 %fusion.11 = s32[16,8,128]{2,1,0:T(8,128)S(1)} fusion(s32[8,128]{1,0:T(8,128)} %bitcast.42), kind=kLoop, calls=%fused_computation.22 | loop fusion | flops 32768 | bytes 69632 | tf_op jit(solution)/shard_map/convert_element_type | solution.py:14
  1.4 4.5 %reduce-window.6 = s32[16,8,128]{2,1,0:T(8,128)S(1)} reduce-window(s32[16,8,128]{2,1,0:T(8,128)S(1)} %fusion.11, s32[]{:T(128)} %constant.5.clone.1), window={size=1x1x128 pad=0_0x0_0x127_0}, to_apply=%region_2.3 | reduce-window | flops 2080768 | bytes 131076 | tf_op jit(solution)/shard_map/reduce-window
  6.3 0.7 %fusion.10 = s32[1024]{0:T(1024)S(1)} fusion(s32[2,8,8,128]{3,2,1,0:T(8,128)S(1)} %bitcast.41, s32[1024]{0:T(1024)} %bitcast.43), kind=kLoop, calls=%fused_computation.19 | loop fusion | flops 48128 | bytes 73728 | tf_op jit(solution)/shard_map/reduce_sum | solution.py:15
  7.0 0.7 %compare_select_fusion = s32[1024,1]{0,1:T(1,128)S(1)} fusion(s32[1024,1]{0,1:T(1,128)S(1)} %bitcast.48, s32[1024,1]{0,1:T(1,128)} %param.7), kind=kLoop, calls=%fused_computation.24 | loop fusion | flops 5120 | bytes 12288 | tf_op jit(solution)/shard_map/select_n | solution.py:52
  7.7 4.3 %scatter_custom_fusion.1 = f32[2048]{0:T(1024)S(1)} fusion(s32[1024]{0:T(1024)S(1)} %bitcast.45, f32[1024]{0:T(1024)S(1)} %broadcast.53, f32[]{:T(128)} %constant.17.clone.1), kind=kCustom, calls=%fused_computation.28 | custom fusion | bytes 8196 | tf_op jit(solution)/shard_map/scatter | solution.py:54
  12.1 33.2 %all_gather.3 = bf16[16,224,64]{1,2,0:T(8,128)(2,1)S(1)} all-gather(bf16[2,224,64]{1,2,0:T(8,128)(2,1)} %param.6), channel_id=1, replica_groups=mesh['blk'=8,'pix'=4] {'blk'}, dimensions={0}, use_global_device_ids=true | all-gather | bytes 516096 | tf_op jit(solution)/shard_map/all_gather | solution.py:55
  45.5 5.3 %scatter_custom_fusion = bf16[2048,224]{1,0:T(8,128)(2,1)S(1)} fusion(s32[1024]{0:T(1024)S(1)} %bitcast.47, bf16[1024,224]{1,0:T(8,128)(2,1)S(1)} %copy.27, bf16[]{:T(256)} %constant.21.clone.1), kind=kCustom, calls=%fused_computation.14 | custom fusion | bytes 917506 | tf_op jit(solution)/shard_map/scatter | solution.py:52
  50.8 0.5 convolution_add_fusion
  51.3 0.6 copy.29
  51.9 0.3 abs_reduce_fusion
  52.4 6.0 %while.11 = (s32[]{:T(128)}, f32[16,128,64]{1,2,0:T(8,128)S(1)}, f32[16]{0:T(128)S(1)}, f32[16,64,64]{1,2,0:T(8,128)S(1)}, f32[16,128,64]{1,2,0:T(8,128)S(1)}, /*index=5*/s32[]{:T(128)}, s32[]{:T(128)}) while((s32[]{:T(128)}, f32[16,128,64]{1,2,0:T(8,128)S(1)}, f32[16]{0:T(128)S(1)}, f32[16,64,64]{1,2,0:T(8,128)S(1)}, ...), condition=%wide.region_7.8_spmd.clone, body=%wide.region_6.7_spmd.clone.sunk | while | flops 101449728 | bytes 2883735 | solution.py:37
  52.4 0.7 fusion.28
  53.2 0.7 fusion.28
  53.9 0.7 fusion.28
  54.7 0.7 fusion.28
  55.4 0.7 fusion.28
  56.2 0.7 fusion.28
  56.9 0.7 fusion.28
  57.7 0.7 fusion.28
  58.4 1.1 %multiply_reduce_fusion = f32[16,128]{1,0:T(8,128)S(1)} fusion(bf16[16,128,224]{1,2,0:T(8,128)(2,1)S(1)} %copy.29, f32[16,128,64]{1,2,0:T(8,128)S(1)} %get-tuple-element.29, bf16[16,224,64]{1,2,0:T(8,128)(2,1)S(1)} %all_gather.3), kind=kOutput, calls=%fused_computation.11 | convolution fusion | flops 354154496 | bytes 1908736 | tf_op jit(solution)/shard_map/nsm,nbm->nsb/dot_general | solution.py:38
  59.6 6.2 %psum.7 = f32[1,16]{1,0:T(1,128)} all-reduce(f32[1,16]{1,0:T(1,128)S(1)} %bitcast.49), channel_id=1, replica_groups=mesh['blk'=8,'pix'=4] {'pix'}, use_global_device_ids=true, to_apply=%region_11.12 | all-reduce | flops 16 | bytes 128 | tf_op jit(solution)/shard_map/psum | solution.py:61
  65.8 0.3 copy.30
  66.1 2.8 %gather_fusion = f32[1024,64]{1,0:T(8,128)S(1)} fusion(f32[2048,64]{1,0:T(8,128)S(1)} %bitcast.38, s32[1024]{0:T(1024)S(1)} %broadcast_clamp_fusion), kind=kCustom, calls=%fused_computation | custom fusion | bytes 528384 | tf_op jit(solution)/shard_map/gather | solution.py:58
  68.9 0.9 %copy.32 = f32[1024,64]{0,1:T(8,128)} copy(f32[1024,64]{1,0:T(8,128)S(1)} %gather_fusion) | data formatting | bytes 524288
  (24 shorter events, 1.1 us)
Async XLA Ops:
  0.6 44.7 %copy-start = (bf16[1024,224]{0,1:T(8,128)(2,1)S(1)}, bf16[1024,224]{0,1:T(8,128)(2,1)}, u32[]{:S(2)}) copy-start(bf16[1024,224]{0,1:T(8,128)(2,1)} %param.5) | copy-start | bytes 1376260
where the time goes:
time: 70.1 us; the launch traced here: 69.8 us
  blocking collectives  39.4 us (56%)
  local copies, waits for them, and re-layouts  15 us (21%)
  matrix products  7.35 us (10%)
  other arithmetic  7.02 us (10%)
  between operations  0.75 us (1%)
    all_gather x1, blocking collectives, per_device(): piece = lax.all_gather(bundles, 'blk', axis=0, tiled=True)  33.2 us
    psum x1, blocking collectives, per_device(): total = lax.psum(energy, 'pix')  6.17 us
    dot_general x8, matrix products, sweep(): jnp.einsum('nsm,nmk->nsk', state, gram, precision=lax.Precision.HIGHEST)  5.45 us
    scatter x1, local copies, waits for them, and re-layouts, per_device(): flat = jnp.zeros((count * cap, bands), jnp.bfloat16).at[slots].set(pixels)  5.28 us
    another operation x3, other arithmetic  4.61 us
    scatter x1, local copies, waits for them, and re-layouts, per_device(): jnp.zeros((count * cap,), jnp.float32).at[slots].set(1.0)  4.32 us
    gather x1, local copies, waits for them, and re-layouts, per_device(): chosen = state.reshape(count * cap, width)[slots]  2.81 us

commit v1 on v0

v1 whole, which is shorter than its diff:
```python
import functools

import jax
import jax.numpy as jnp
from jax import lax
from jax.experimental import pallas as pl
from jax.experimental.pallas import tpu as pltpu
from jax.sharding import PartitionSpec as P

ITERS = 8
MESH = pl.DeviceIdType.MESH
LANES = 128
TILE = 256

sum_weight = 0.015625


def split(value):
    high = value.astype(jnp.bfloat16)
    low = (value - high.astype(jnp.float32)).astype(jnp.bfloat16)
    return high, low


def mask(cond):
    return jnp.where(cond, 1.0, 0.0).astype(jnp.bfloat16)


def dot(a, b, dims=((1,), (0,))):
    return lax.dot_general(a, b, (dims, ((), ())), preferred_element_type=jnp.float32)


def kernel(
    dims, label_ref, pix_hbm, bun_hbm, out_hbm, energy_ref,
    pix, own, spectra, slots, counts, pick, part, m_ref, c_ref, a_ref, packed, out, sums,
    local_sem, out_sem, send_sem, recv_sem, esend_sem, erecv_sem,
):
    n_blk, n_pix = dims
    me, my = lax.axis_index("blk"), lax.axis_index("pix")
    rows, bands = pix.shape
    owned, _, width = own.shape
    count = n_blk * owned
    cap = 2 * rows // count
    per = TILE // width
    groups = count // per
    packed_rows = groups * cap

    get_bun = pltpu.make_async_copy(bun_hbm, own, local_sem.at[0])
    get_pix = pltpu.make_async_copy(pix_hbm, pix, local_sem.at[1])
    get_bun.start()
    get_pix.start()

    barrier = pltpu.get_barrier_semaphore()
    for o in range(1, n_blk):
        pl.semaphore_signal(
            barrier, inc=1, device_id=(lax.rem(me + o, n_blk), my), device_id_type=MESH
        )
    for o in range(1, n_pix):
        pl.semaphore_signal(
            barrier, inc=1, device_id=(me, lax.rem(my + o, n_pix)), device_id_type=MESH
        )
    get_bun.wait()
    spectra[me] = jnp.concatenate([own[i] for i in range(owned)], axis=1)
    pl.semaphore_wait(barrier, n_blk + n_pix - 2)

    def bundle_copy(o, slot):
        return pltpu.make_async_remote_copy(
            src_ref=spectra.at[slot],
            dst_ref=spectra.at[slot],
            send_sem=send_sem.at[o],
            recv_sem=recv_sem.at[o],
            device_id=(lax.rem(me + o, n_blk), my),
            device_id_type=MESH,
        )

    for o in range(1, n_blk):
        bundle_copy(o, me).start()

    label = label_ref[...]
    kinds = lax.broadcasted_iota(jnp.int32, (count, TILE), 0)
    blocks = rows // TILE
    hot = [
        jnp.where(label[:, b * TILE:(b + 1) * TILE] == kinds, 1.0, 0.0) for b in range(blocks)
    ]
    upper = mask(
        lax.broadcasted_iota(jnp.int32, (TILE, TILE), 0)
        <= lax.broadcasted_iota(jnp.int32, (TILE, TILE), 1)
    )
    run = dot(jnp.concatenate(hot, axis=0).astype(jnp.bfloat16), upper)
    carry = jnp.zeros((count, 1), jnp.float32)
    ranks = []
    for b in range(blocks):
        here = run[b * count:(b + 1) * count]
        ranks.append(jnp.sum(hot[b] * (here + carry), axis=0, keepdims=True) - 1.0)
        carry = carry + here[:, TILE - 1:TILE]
    counts[...] = jnp.broadcast_to(carry, counts.shape)
    rank = jnp.concatenate(ranks, axis=1)
    shift = per.bit_length() - 1
    slot = label.astype(jnp.float32) * float(cap) + rank
    place = (label >> shift).astype(jnp.float32) * float(cap) + rank
    piece = (label & (per - 1)).astype(jnp.float32)

    get_pix.wait()
    step_rows = 512
    for s in range(count * cap // step_rows):
        index = lax.broadcasted_iota(jnp.int32, (step_rows, rows), 0) + s * step_rows
        chosen = mask(slot == index.astype(jnp.float32))
        slots[s * step_rows:(s + 1) * step_rows] = dot(chosen, pix[...]).astype(jnp.bfloat16)

    place_t = jnp.broadcast_to(place, (LANES, rows)).T
    part[...] = jnp.broadcast_to(piece, (LANES, rows)).T
    for s in range(packed_rows // LANES):
        index = lax.broadcasted_iota(jnp.int32, (rows, LANES), 1) + s * LANES
        pick[:, s * LANES:(s + 1) * LANES] = mask(place_t == index.astype(jnp.float32))

    for o in range(1, n_blk):
        bundle_copy(o, lax.rem(me + n_blk - o, n_blk)).wait_recv()

    together = min(groups, 4)
    lane = lax.broadcasted_iota(jnp.int32, (1, TILE), 1)
    seg = lane // width
    seg_rows = lax.broadcasted_iota(jnp.int32, (TILE, TILE), 0) // width
    seg_cols = lax.broadcasted_iota(jnp.int32, (TILE, TILE), 1) // width
    hold = TILE // (owned * width)
    half = lax.broadcasted_iota(jnp.int32, (1, LANES), 1) // width
    in_half = LANES // width
    row_of = lax.broadcasted_iota(jnp.int32, (cap, TILE), 0).astype(jnp.float32)
    energy_lane = lax.broadcasted_iota(jnp.int32, (1, LANES), 1)

    def group_spectra(g):
        return jnp.concatenate([spectra[g * hold + i] for i in range(hold)], axis=1)

    def solve(c, energy):
        for i in range(together):
            g = c * together + i
            both = group_spectra(g)
            gram = dot(both, both, ((0,), (0,))) + sum_weight
            gram = jnp.where(seg_rows == seg_cols, gram, 0.0)
            total = jnp.sum(jnp.abs(gram), axis=0, keepdims=True)
            step = jnp.zeros_like(total)
            for j in range(per):
                top = jnp.max(jnp.where(seg == j, total, 0.0), axis=1, keepdims=True)
                step = jnp.where(seg == j, 1.0 / top, step)
            high, low = split(gram * step)
            m_ref[i, 0:TILE] = high
            m_ref[i, TILE:2 * TILE] = high
            m_ref[i, 2 * TILE:3 * TILE] = low
            raw = dot(slots[pl.ds(g * per * cap, per * cap)], both)
            target = raw[0:cap]
            for j in range(1, per):
                target = jnp.where(seg == j, raw[j * cap:(j + 1) * cap], target)
            moved = step * (target + sum_weight)
            c_ref[i] = moved
            a_ref[i] = jnp.maximum(moved, 0.0)
        for _ in range(ITERS - 1):
            for i in range(together):
                state = a_ref[i]
                high, low = split(state)
                grad = dot(jnp.concatenate([high, low, high], axis=1), m_ref[i])
                a_ref[i] = jnp.maximum(state - grad + c_ref[i], 0.0)
        for i in range(together):
            g = c * together + i
            state = a_ref[i]
            high, low = split(state)
            packed[pl.ds(g * cap, cap)] = high
            packed[pl.ds(packed_rows + g * cap, cap)] = low
            tops = [counts[pl.ds(g * per + j, 1), :] for j in range(per)]
            spans = []
            for h in range(per // in_half):
                span = tops[h * in_half]
                for j in range(1, in_half):
                    span = jnp.where(half == j, tops[h * in_half + j], span)
                spans.append(span)
            kept = jnp.where(row_of < jnp.concatenate(spans, axis=1), state, 0.0)
            high, low = split(
                jnp.concatenate([jnp.where(seg == j, kept, 0.0) for j in range(per)], axis=0)
            )
            both = group_spectra(g)
            fitted = dot(high, both, ((1,), (1,))) + dot(low, both, ((1,), (1,)))
            misfit = slots[pl.ds(g * per * cap, per * cap)].astype(jnp.float32) - fitted
            square = misfit * misfit
            for j in range(per):
                column = jnp.sum(square[j * cap:(j + 1) * cap], axis=0, keepdims=True)
                value = jnp.sum(column, axis=1, keepdims=True)
                energy = jnp.where(energy_lane == g * per + j, value, energy)
        return energy

    energy = jnp.zeros((1, LANES), jnp.float32)
    if groups == together:
        energy = solve(0, energy)
    else:
        energy = lax.fori_loop(0, groups // together, solve, energy)
    scale = bands * rows * n_pix / count
    sums[my] = jnp.broadcast_to(energy * (1.0 / scale), sums.shape[1:])

    def energy_copy(o, which):
        return pltpu.make_async_remote_copy(
            src_ref=sums.at[which],
            dst_ref=sums.at[which],
            send_sem=esend_sem.at[o],
            recv_sem=erecv_sem.at[o],
            device_id=(me, lax.rem(my + o, n_pix)),
            device_id_type=MESH,
        )

    def put(r):
        cut = pl.ds(r * TILE, TILE)
        return pltpu.make_async_copy(out.at[cut], out_hbm.at[cut], out_sem.at[r])

    def unsort(r):
        cut = slice(r * TILE, (r + 1) * TILE)
        one = pick[cut]
        wide = dot(jnp.concatenate([one, one], axis=1), packed[...])
        where_ = part[cut]
        value = jnp.zeros((TILE, width), jnp.float32)
        for h in range(per // in_half):
            block = wide[:, h * LANES:(h + 1) * LANES]
            for j in range(in_half):
                shifted = block if j == 0 else pltpu.roll(block, LANES - j * width, 1)
                value = jnp.where(
                    where_[:, :width] == float(h * in_half + j), shifted[:, :width], value
                )
        out[cut] = value
        put(r).start()

    for r in range(rows // TILE):
        unsort(r)
        if r == 0:
            for o in range(1, n_pix):
                energy_copy(o, my).start()
    for o in range(1, n_pix):
        energy_copy(o, lax.rem(my + n_pix - o, n_pix)).wait_recv()
    total = sums[0]
    for i in range(1, n_pix):
        total = total + sums[i]
    energy_ref[...] = total[0:1, :count]
    for o in range(1, n_pix):
        energy_copy(o, my).wait_send()
    for o in range(1, n_blk):
        bundle_copy(o, me).wait_send()
    for r in range(rows // TILE):
        put(r).wait()


def per_device(pixels, bundles, assign):
    rows, bands = pixels.shape
    owned, _, width = bundles.shape
    n_blk, n_pix = lax.axis_size("blk"), lax.axis_size("pix")
    count = n_blk * owned
    cap = 2 * rows // count
    per = TILE // width
    groups = count // per
    together = min(groups, 4)
    packed_rows = groups * cap
    any_space = pl.BlockSpec(memory_space=pl.ANY)
    vmem = pl.BlockSpec(memory_space=pltpu.VMEM)
    return pl.pallas_call(
        functools.partial(kernel, (n_blk, n_pix)),
        out_shape=(
            jax.ShapeDtypeStruct((rows, width), jnp.float32),
            jax.ShapeDtypeStruct((1, count), jnp.float32),
        ),
        in_specs=[vmem, any_space, any_space],
        out_specs=(any_space, vmem),
        scratch_shapes=[
            pltpu.VMEM((rows, bands), jnp.bfloat16),
            pltpu.VMEM((owned, bands, width), jnp.bfloat16),
            pltpu.VMEM((n_blk, bands, owned * width), jnp.bfloat16),
            pltpu.VMEM((count * cap, bands), jnp.bfloat16),
            pltpu.VMEM((count, LANES), jnp.float32),
            pltpu.VMEM((rows, packed_rows), jnp.bfloat16),
            pltpu.VMEM((rows, LANES), jnp.float32),
            pltpu.VMEM((together, 3 * TILE, TILE), jnp.bfloat16),
            pltpu.VMEM((together, cap, TILE), jnp.float32),
            pltpu.VMEM((together, cap, TILE), jnp.float32),
            pltpu.VMEM((2 * packed_rows, TILE), jnp.bfloat16),
            pltpu.VMEM((rows, width), jnp.float32),
            pltpu.VMEM((n_pix, 8, LANES), jnp.float32),
            pltpu.SemaphoreType.DMA((2,)),
            pltpu.SemaphoreType.DMA((rows // TILE,)),
            pltpu.SemaphoreType.DMA((n_blk,)),
            pltpu.SemaphoreType.DMA((n_blk,)),
            pltpu.SemaphoreType.DMA((n_pix,)),
            pltpu.SemaphoreType.DMA((n_pix,)),
        ],
        compiler_params=pltpu.CompilerParams(collective_id=0, has_side_effects=True),
        name="unmix",
    )(assign.reshape(1, rows), pixels, bundles)


def solution(mesh):
    placed = (P(("blk", "pix"), None), P("blk", None, None), P(("blk", "pix"), None))
    return jax.shard_map(
        per_device,
        mesh=mesh,
        in_specs=placed,
        out_specs=(P(("blk", "pix"), None), P("blk", None)),
        check_vma=False,
    )
```

time: 70.1 us -> 29.3 us (0.42)
  the two profiles are of different devices: /device:TPU:0 before, /device:TPU:13 now
where the time goes in v1:
time: 29.3 us; the launch traced here: 29 us
  Pallas kernels  22.4 us (76%)
  local copies, waits for them, and re-layouts  6.04 us (21%)
  between operations  0.65 us (2%)
    pallas_call x1, Pallas kernels, per_device(): pl.pallas_call(functools.partial(kernel, (n_blk, n_pix)), out_shape=(jax....  22.4 us
    unnamed x5, local copies, waits for them, and re-layouts  4.11 us
    pallas_call x1, local copies, waits for them, and re-layouts, per_device(): pl.pallas_call(functools.partial(kernel, (n_blk, n_pix)), out_shape=(jax....  1.93 us

profile of v1, /device:TPU:13, one launch (start us, length us, event | category | flops | bytes accessed | tf_op | source)
XLA Modules:
  0.0 29.0 jit_solution(11830038099397520700)
XLA Ops:
  0.6 1.6 %copy.6.bun_hbm = bf16[2,224,64]{2,1,0:T(8,128)(2,1)} copy(bf16[2,224,64]{1,2,0:T(8,128)(2,1)} %param.4) | data formatting | bytes 114688 | tf_op args[1]
  2.2 2.0 %copy.5.pix_hbm = bf16[1024,224]{1,0:T(8,128)(2,1)} copy(bf16[1024,224]{0,1:T(8,128)(2,1)} %param.3) | data formatting | bytes 917504 | tf_op args[0]
  4.2 22.4 %unmix.1 = (f32[1024,64]{1,0:T(8,128)}, f32[1,16]{1,0:T(1,128)}) custom-call(s32[1,1024]{1,0:T(1,128)} %bitcast.1, bf16[1024,224]{1,0:T(8,128)(2,1)} %copy.5.pix_hbm, bf16[2,224,64]{2,1,0:T(8,128)(2,1)} %copy.6.bun_hbm), custom_call_target="tpu_custom_call" | custom-call | tf_op jit(solution)/shard_map/unmix/pallas_call | solution.py:256
  26.6 0.0 copy-start
  26.6 1.9 %copy.7 = f32[1024,64]{0,1:T(8,128)} copy(f32[1024,64]{1,0:T(8,128)} %get-tuple-element.2) | data formatting | bytes 524288 | tf_op jit(solution)/shard_map/unmix/pallas_call | solution.py:256
  28.5 0.0 copy-done
  28.5 0.5 %copy.9 = f32[1,16]{1,0:T(1,128)} copy(f32[1,16]{1,0:T(1,128)S(1)} %copy-done) | data formatting | bytes 128
Async XLA Ops:
  26.6 1.9 %copy-start = (f32[1,16]{1,0:T(1,128)S(1)}, f32[1,16]{1,0:T(1,128)}, u32[]{:S(2)}) copy-start(f32[1,16]{1,0:T(1,128)} %get-tuple-element.7) | copy-start | bytes 196

commit v2 on v1

v2 whole, which is shorter than its diff:
```python
import functools

import jax
import jax.numpy as jnp
from jax import lax
from jax.experimental import pallas as pl
from jax.experimental.pallas import tpu as pltpu
from jax.sharding import PartitionSpec as P

ITERS = 8
MESH = pl.DeviceIdType.MESH
LANES = 128
TILE = 256

sum_weight = 0.015625
ACROSS = ((1,), (1,))


def split(value):
    high = value.astype(jnp.bfloat16)
    low = (value - high.astype(jnp.float32)).astype(jnp.bfloat16)
    return high, low


def mask(cond):
    return jnp.where(cond, 1.0, 0.0).astype(jnp.bfloat16)


def dot(a, b, dims=((1,), (0,))):
    return lax.dot_general(a, b, (dims, ((), ())), preferred_element_type=jnp.float32)


def kernel(
    dims, label_ref, pix_hbm, bun_hbm, out_hbm, energy_ref,
    pix, spectra, slots, counts, pick, m_ref, c_ref, a_ref, packed, turned, out, sums,
    local_sem, out_sem, send_sem, recv_sem, esend_sem, erecv_sem,
):
    n_blk, n_pix, owned = dims
    me, my = lax.axis_index("blk"), lax.axis_index("pix")
    bands, rows = pix.shape
    piece_rows = bun_hbm.shape[0]
    width = piece_rows // owned
    count = n_blk * owned
    cap = 2 * rows // count
    per = TILE // width
    groups = count // per
    packed_rows = groups * cap
    hold = n_blk // groups
    together = min(groups, 4)
    z, y = me // hold, lax.rem(me, hold)

    def piece_at(device):
        return spectra.at[pl.ds(device * piece_rows, piece_rows)]

    get_bun = pltpu.make_async_copy(bun_hbm, piece_at(me), local_sem.at[0])
    get_pix = pltpu.make_async_copy(pix_hbm, pix, local_sem.at[1])
    get_bun.start()
    get_pix.start()

    barrier = pltpu.get_barrier_semaphore()
    for o in range(1, n_blk):
        pl.semaphore_signal(
            barrier, inc=1, device_id=(lax.rem(me + o, n_blk), my), device_id_type=MESH
        )
    for o in range(1, n_pix):
        pl.semaphore_signal(
            barrier, inc=1, device_id=(me, lax.rem(my + o, n_pix)), device_id_type=MESH
        )

    label = label_ref[...]
    kinds = lax.broadcasted_iota(jnp.int32, (count, TILE), 0)
    blocks = rows // TILE
    hot = [
        jnp.where(label[:, b * TILE:(b + 1) * TILE] == kinds, 1.0, 0.0) for b in range(blocks)
    ]
    upper = mask(
        lax.broadcasted_iota(jnp.int32, (TILE, TILE), 0)
        <= lax.broadcasted_iota(jnp.int32, (TILE, TILE), 1)
    )
    run = dot(jnp.concatenate(hot, axis=0).astype(jnp.bfloat16), upper)
    carry = jnp.zeros((count, 1), jnp.float32)
    ranks = []
    for b in range(blocks):
        here = run[b * count:(b + 1) * count]
        ranks.append(jnp.sum(hot[b] * (here + carry), axis=0, keepdims=True) - 1.0)
        carry = carry + here[:, TILE - 1:TILE]
    counts[...] = jnp.broadcast_to(carry, counts.shape)
    rank = jnp.concatenate(ranks, axis=1)
    shift = per.bit_length() - 1
    slot = label.astype(jnp.float32) * float(cap) + rank
    place = (label >> shift).astype(jnp.float32) * float(cap) + rank
    part = label & (per - 1)
    for s in range(packed_rows // LANES):
        index = lax.broadcasted_iota(jnp.int32, (LANES, rows), 0) + s * LANES
        pick[s * LANES:(s + 1) * LANES] = mask(place == index.astype(jnp.float32))

    get_bun.wait()
    pl.semaphore_wait(barrier, n_blk + n_pix - 2)

    def bundle_copy(dz, dy, which):
        peer = lax.rem(z + dz, groups) * hold + lax.rem(y + dy, hold)
        return pltpu.make_async_remote_copy(
            src_ref=piece_at(which),
            dst_ref=piece_at(which),
            send_sem=send_sem.at[dz * hold + dy],
            recv_sem=recv_sem.at[dz * hold + dy],
            device_id=(peer, my),
            device_id_type=MESH,
        )

    def arrived(dz):
        for dy in range(hold):
            if dz or dy:
                source = lax.rem(z + groups - dz, groups) * hold + lax.rem(y + hold - dy, hold)
                bundle_copy(dz, dy, source).wait_recv()

    order = sorted(range(groups), key=lambda dz: min(dz, groups - dz))
    others = [(dz, dy) for dz in order for dy in range(hold) if dz or dy]
    for dz, dy in others:
        bundle_copy(dz, dy, me).start()

    get_pix.wait()
    step_rows = 512
    for s in range(count * cap // step_rows):
        index = lax.broadcasted_iota(jnp.int32, (step_rows, rows), 0) + s * step_rows
        chosen = mask(slot == index.astype(jnp.float32))
        slots[s * step_rows:(s + 1) * step_rows] = dot(chosen, pix[...], ACROSS).astype(
            jnp.bfloat16
        )

    lane = lax.broadcasted_iota(jnp.int32, (1, TILE), 1)
    seg = lane // width
    seg_rows = lax.broadcasted_iota(jnp.int32, (TILE, TILE), 0) // width
    seg_cols = lax.broadcasted_iota(jnp.int32, (TILE, TILE), 1) // width
    half = lax.broadcasted_iota(jnp.int32, (1, LANES), 1) // width
    in_half = LANES // width
    row_of = lax.broadcasted_iota(jnp.int32, (cap, TILE), 0).astype(jnp.float32)
    energy_lane = lax.broadcasted_iota(jnp.int32, (1, LANES), 1)

    def group_spectra(g):
        return spectra[pl.ds(g * TILE, TILE)]

    def prepare(i, g):
        both = group_spectra(g)
        gram = dot(both, both, ACROSS) + sum_weight
        gram = jnp.where(seg_rows == seg_cols, gram, 0.0)
        total = jnp.sum(jnp.abs(gram), axis=0, keepdims=True)
        step = jnp.zeros_like(total)
        for j in range(per):
            top = jnp.max(jnp.where(seg == j, total, 0.0), axis=1, keepdims=True)
            step = jnp.where(seg == j, 1.0 / top, step)
        high, low = split(gram * step)
        m_ref[i, 0:TILE] = high
        m_ref[i, TILE:2 * TILE] = high
        m_ref[i, 2 * TILE:3 * TILE] = low
        raw = dot(slots[pl.ds(g * per * cap, per * cap)], both, ACROSS)
        target = raw[0:cap]
        for j in range(1, per):
            target = jnp.where(seg == j, raw[j * cap:(j + 1) * cap], target)
        moved = step * (target + sum_weight)
        c_ref[i] = moved
        a_ref[i] = jnp.maximum(moved, 0.0)

    def iterate(which):
        for _ in range(ITERS - 1):
            for i in which:
                state = a_ref[i]
                high, low = split(state)
                grad = dot(jnp.concatenate([high, low, high], axis=1), m_ref[i])
                a_ref[i] = jnp.maximum(state - grad + c_ref[i], 0.0)

    def finish(i, g, energy):
        state = a_ref[i]
        packed[pl.ds(g * cap, cap)] = state
        tops = [counts[pl.ds(g * per + j, 1), :] for j in range(per)]
        spans = []
        for h in range(per // in_half):
            span = tops[h * in_half]
            for j in range(1, in_half):
                span = jnp.where(half == j, tops[h * in_half + j], span)
            spans.append(span)
        kept = jnp.where(row_of < jnp.concatenate(spans, axis=1), state, 0.0)
        high, low = split(
            jnp.concatenate([jnp.where(seg == j, kept, 0.0) for j in range(per)], axis=0)
        )
        both = group_spectra(g)
        fitted = dot(high, both) + dot(low, both)
        misfit = slots[pl.ds(g * per * cap, per * cap)].astype(jnp.float32) - fitted
        square = misfit * misfit
        for j in range(per):
            column = jnp.sum(square[j * cap:(j + 1) * cap], axis=0, keepdims=True)
            value = jnp.sum(column, axis=1, keepdims=True)
            energy = jnp.where(energy_lane == g * per + j, value, energy)
        return energy

    energy = jnp.zeros((1, LANES), jnp.float32)
    if groups == together:
        numbers = [lax.rem(z + groups - dz, groups) for dz in order]
        for i, dz in enumerate(order):
            arrived(dz)
            prepare(i, numbers[i])
        iterate(range(groups))
        for i in range(groups):
            energy = finish(i, numbers[i], energy)
    else:
        for dz in order:
            arrived(dz)

        def chunk(c, energy):
            for i in range(together):
                prepare(i, c * together + i)
            iterate(range(together))
            for i in range(together):
                energy = finish(i, c * together + i, energy)
            return energy

        energy = lax.fori_loop(0, groups // together, chunk, energy)
    scale = bands * rows * n_pix / count
    sums[my] = jnp.broadcast_to(energy * (1.0 / scale), sums.shape[1:])

    def energy_copy(o, which):
        return pltpu.make_async_remote_copy(
            src_ref=sums.at[which],
            dst_ref=sums.at[which],
            send_sem=esend_sem.at[o],
            recv_sem=erecv_sem.at[o],
            device_id=(me, lax.rem(my + o, n_pix)),
            device_id_type=MESH,
        )

    high, low = split(packed[...].T)
    turned[0:TILE] = high
    turned[TILE:2 * TILE] = low
    for o in range(1, n_pix):
        energy_copy(o, my).start()

    def put(r):
        cut = pl.ds(r * TILE, TILE)
        return pltpu.make_async_copy(out.at[:, cut], out_hbm.at[:, cut], out_sem.at[r])

    for r in range(rows // TILE):
        cut = slice(r * TILE, (r + 1) * TILE)
        pair = dot(turned[...], pick[:, cut])
        wide = pair[:TILE] + pair[TILE:]
        which = part[:, cut]
        value = wide[0:width]
        for j in range(1, per):
            value = jnp.where(which == j, wide[j * width:(j + 1) * width], value)
        out[:, cut] = value
        put(r).start()

    for o in range(1, n_pix):
        energy_copy(o, lax.rem(my + n_pix - o, n_pix)).wait_recv()
    total = sums[0]
    for i in range(1, n_pix):
        total = total + sums[i]
    energy_ref[...] = total[0:1, :count]
    for o in range(1, n_pix):
        energy_copy(o, my).wait_send()
    for dz, dy in others:
        bundle_copy(dz, dy, me).wait_send()
    for r in range(rows // TILE):
        put(r).wait()


def per_device(pixels, bundles, assign):
    rows, bands = pixels.shape
    owned, _, width = bundles.shape
    n_blk, n_pix = lax.axis_size("blk"), lax.axis_size("pix")
    count = n_blk * owned
    cap = 2 * rows // count
    per = TILE // width
    groups = count // per
    together = min(groups, 4)
    packed_rows = groups * cap
    any_space = pl.BlockSpec(memory_space=pl.ANY)
    vmem = pl.BlockSpec(memory_space=pltpu.VMEM)
    abundances, energy = pl.pallas_call(
        functools.partial(kernel, (n_blk, n_pix, owned)),
        out_shape=(
            jax.ShapeDtypeStruct((width, rows), jnp.float32),
            jax.ShapeDtypeStruct((1, count), jnp.float32),
        ),
        in_specs=[vmem, any_space, any_space],
        out_specs=(any_space, vmem),
        scratch_shapes=[
            pltpu.VMEM((bands, rows), jnp.bfloat16),
            pltpu.VMEM((count * width, bands), jnp.bfloat16),
            pltpu.VMEM((count * cap, bands), jnp.bfloat16),
            pltpu.VMEM((count, LANES), jnp.float32),
            pltpu.VMEM((packed_rows, rows), jnp.bfloat16),
            pltpu.VMEM((together, 3 * TILE, TILE), jnp.bfloat16),
            pltpu.VMEM((together, cap, TILE), jnp.float32),
            pltpu.VMEM((together, cap, TILE), jnp.float32),
            pltpu.VMEM((packed_rows, TILE), jnp.float32),
            pltpu.VMEM((2 * TILE, packed_rows), jnp.bfloat16),
            pltpu.VMEM((width, rows), jnp.float32),
            pltpu.VMEM((n_pix, 8, LANES), jnp.float32),
            pltpu.SemaphoreType.DMA((2,)),
            pltpu.SemaphoreType.DMA((rows // TILE,)),
            pltpu.SemaphoreType.DMA((n_blk,)),
            pltpu.SemaphoreType.DMA((n_blk,)),
            pltpu.SemaphoreType.DMA((n_pix,)),
            pltpu.SemaphoreType.DMA((n_pix,)),
        ],
        compiler_params=pltpu.CompilerParams(collective_id=0, has_side_effects=True),
        name="unmix",
    )(
        assign.reshape(1, rows),
        pixels.T,
        bundles.transpose(0, 2, 1).reshape(owned * width, bands),
    )
    return abundances.T, energy


def solution(mesh):
    placed = (P(("blk", "pix"), None), P("blk", None, None), P(("blk", "pix"), None))
    return jax.shard_map(
        per_device,
        mesh=mesh,
        in_specs=placed,
        out_specs=(P(("blk", "pix"), None), P("blk", None)),
        check_vma=False,
    )
```

time: 29.3 us -> 28.5 us (0.973)
  the two profiles are of different devices: /device:TPU:13 before, /device:TPU:0 now
where the time goes in v2:
time: 28.5 us; the launch traced here: 28.4 us
  Pallas kernels  25.5 us (89%)
  local copies, waits for them, and re-layouts  2.19 us (8%)
  between operations  0.65 us (2%)
    pallas_call x1, Pallas kernels, per_device(): pl.pallas_call(functools.partial(kernel, (n_blk, n_pix, owned)), out_shap...  25.5 us
    unnamed x4, local copies, waits for them, and re-layouts  2.19 us

profile of v2, /device:TPU:0, one launch (start us, length us, event | category | flops | bytes accessed | tf_op | source)
XLA Modules:
  0.0 28.4 jit_solution(3081963153570014731)
XLA Ops:
  0.6 25.5 %unmix.1 = (f32[64,1024]{1,0:T(8,128)}, f32[1,16]{1,0:T(1,128)}) custom-call(s32[1,1024]{1,0:T(1,128)} %bitcast.9, bf16[224,1024]{1,0:T(8,128)(2,1)} %bitcast.6, bf16[128,224]{1,0:T(8,128)(2,1)} %bitcast.8), custom_call_target="tpu_custom_call" | custom-call | tf_op jit(solution)/shard_map/unmix/pallas_call | solution.py:278
  26.2 0.0 copy-start
  26.2 1.7 %copy.7 = f32[1024,64]{0,1:T(8,128)} copy(f32[1024,64]{0,1:T(8,128)} %bitcast.7) | data formatting | bytes 524288
  27.8 0.0 copy-done
  27.9 0.5 %copy.8 = f32[1,16]{1,0:T(1,128)} copy(f32[1,16]{1,0:T(1,128)S(1)} %copy-done) | data formatting | bytes 128
Async XLA Ops:
  26.2 1.7 %copy-start = (f32[1,16]{1,0:T(1,128)S(1)}, f32[1,16]{1,0:T(1,128)}, u32[]{:S(2)}) copy-start(f32[1,16]{1,0:T(1,128)} %get-tuple-element.9) | copy-start | bytes 196

commit v3 on v2

--- a/solution.py
+++ b/solution.py
@@ -32,7 +32,7 @@
 
 def kernel(
     dims, label_ref, pix_hbm, bun_hbm, out_hbm, energy_ref,
-    pix, spectra, slots, counts, pick, m_ref, c_ref, a_ref, packed, turned, out, sums,
+    pix, own, spectra, slots, counts, pick, m_ref, c_ref, a_ref, packed, turned, out, sums,
     local_sem, out_sem, send_sem, recv_sem, esend_sem, erecv_sem,
 ):
     n_blk, n_pix, owned = dims
@@ -50,9 +50,9 @@
     z, y = me // hold, lax.rem(me, hold)
 
     def piece_at(device):
-        return spectra.at[pl.ds(device * piece_rows, piece_rows)]
-
-    get_bun = pltpu.make_async_copy(bun_hbm, piece_at(me), local_sem.at[0])
+        return spectra.at[device]
+
+    get_bun = pltpu.make_async_copy(bun_hbm, own, local_sem.at[0])
     get_pix = pltpu.make_async_copy(pix_hbm, pix, local_sem.at[1])
     get_bun.start()
     get_pix.start()
@@ -66,6 +66,9 @@
         pl.semaphore_signal(
             barrier, inc=1, device_id=(me, lax.rem(my + o, n_pix)), device_id_type=MESH
         )
+
+    get_bun.wait()
+    spectra[me] = own[...].astype(jnp.float32).T.astype(jnp.bfloat16)
 
     label = label_ref[...]
     kinds = lax.broadcasted_iota(jnp.int32, (count, TILE), 0)
@@ -94,7 +97,6 @@
         index = lax.broadcasted_iota(jnp.int32, (LANES, rows), 0) + s * LANES
         pick[s * LANES:(s + 1) * LANES] = mask(place == index.astype(jnp.float32))
 
-    get_bun.wait()
     pl.semaphore_wait(barrier, n_blk + n_pix - 2)
 
     def bundle_copy(dz, dy, which):
@@ -138,11 +140,11 @@
     energy_lane = lax.broadcasted_iota(jnp.int32, (1, LANES), 1)
 
     def group_spectra(g):
-        return spectra[pl.ds(g * TILE, TILE)]
+        return jnp.concatenate([spectra[g * hold + i] for i in range(hold)], axis=1)
 
     def prepare(i, g):
         both = group_spectra(g)
-        gram = dot(both, both, ACROSS) + sum_weight
+        gram = dot(both, both, ((0,), (0,))) + sum_weight
         gram = jnp.where(seg_rows == seg_cols, gram, 0.0)
         total = jnp.sum(jnp.abs(gram), axis=0, keepdims=True)
         step = jnp.zeros_like(total)
@@ -153,7 +155,7 @@
         m_ref[i, 0:TILE] = high
         m_ref[i, TILE:2 * TILE] = high
         m_ref[i, 2 * TILE:3 * TILE] = low
-        raw = dot(slots[pl.ds(g * per * cap, per * cap)], both, ACROSS)
+        raw = dot(slots[pl.ds(g * per * cap, per * cap)], both)
         target = raw[0:cap]
         for j in range(1, per):
             target = jnp.where(seg == j, raw[j * cap:(j + 1) * cap], target)
@@ -184,7 +186,7 @@
             jnp.concatenate([jnp.where(seg == j, kept, 0.0) for j in range(per)], axis=0)
         )
         both = group_spectra(g)
-        fitted = dot(high, both) + dot(low, both)
+        fitted = dot(high, both, ACROSS) + dot(low, both, ACROSS)
         misfit = slots[pl.ds(g * per * cap, per * cap)].astype(jnp.float32) - fitted
         square = misfit * misfit
         for j in range(per):
@@ -285,7 +287,8 @@
         out_specs=(any_space, vmem),
         scratch_shapes=[
             pltpu.VMEM((bands, rows), jnp.bfloat16),
-            pltpu.VMEM((count * width, bands), jnp.bfloat16),
+            pltpu.VMEM((owned * width, bands), jnp.bfloat16),
+            pltpu.VMEM((n_blk, bands, owned * width), jnp.bfloat16),
             pltpu.VMEM((count * cap, bands), jnp.bfloat16),
             pltpu.VMEM((count, LANES), jnp.float32),
             pltpu.VMEM((packed_rows, rows), jnp.bfloat16),

time: 28.5 us -> 27 us (0.947)
  Pallas kernels: 25.5 us -> 24 us
    pallas_call x1, Pallas kernels: 25.5 us -> 24 us  [per_device(): pl.pallas_call(functools.partial(kernel, (n_blk, n_pix, owned)), out_shap...]
where the time goes in v3:
time: 27 us; the launch traced here: 26.9 us
  Pallas kernels  24 us (89%)
  local copies, waits for them, and re-layouts  2.19 us (8%)
  between operations  0.65 us (2%)
    pallas_call x1, Pallas kernels, per_device(): pl.pallas_call(functools.partial(kernel, (n_blk, n_pix, owned)), out_shap...  24 us
    unnamed x4, local copies, waits for them, and re-layouts  2.19 us

profile of v3, /device:TPU:0, one launch (start us, length us, event | category | flops | bytes accessed | tf_op | source)
XLA Modules:
  0.0 26.9 jit_solution(11259214025622155089)
XLA Ops:
  0.6 24.0 %unmix.1 = (f32[64,1024]{1,0:T(8,128)}, f32[1,16]{1,0:T(1,128)}) custom-call(s32[1,1024]{1,0:T(1,128)} %bitcast.9, bf16[224,1024]{1,0:T(8,128)(2,1)} %bitcast.6, bf16[128,224]{1,0:T(8,128)(2,1)} %bitcast.8), custom_call_target="tpu_custom_call" | custom-call | tf_op jit(solution)/shard_map/unmix/pallas_call | solution.py:280
  24.7 0.0 copy-start
  24.7 1.7 %copy.7 = f32[1024,64]{0,1:T(8,128)} copy(f32[1024,64]{0,1:T(8,128)} %bitcast.7) | data formatting | bytes 524288
  26.3 0.0 copy-done
  26.4 0.5 %copy.8 = f32[1,16]{1,0:T(1,128)} copy(f32[1,16]{1,0:T(1,128)S(1)} %copy-done) | data formatting | bytes 128
Async XLA Ops:
  24.7 1.7 %copy-start = (f32[1,16]{1,0:T(1,128)S(1)}, f32[1,16]{1,0:T(1,128)}, u32[]{:S(2)}) copy-start(f32[1,16]{1,0:T(1,128)} %get-tuple-element.9) | copy-start | bytes 196
